TPU v7x, 512 devices: a whole 4x8x8 slice. The times are simulated.
512 devices in a mesh: pipe: 16 (over y, core), tensor: 32 (over z, x).
Axes of the slice: x: 4, y: 8, z: 8, core: 2. Of those that a mesh axis runs over, the one named last changes fastest.
Arguments:
- patches: bfloat16 [262144, 1280], P(('pipe', 'tensor')), may hold values from -6 to 6
- attn_gain: float32 [1280], replicated, may hold values from 0.25 to 1.75
- w_qkv: bfloat16 [1280, 3840], P('tensor', 'pipe'), may hold values from -0.1118034 to 0.1118034
- w_out: bfloat16 [1280, 1280], P('tensor', 'pipe'), may hold values from -0.15625 to 0.15625
- merge_gain: float32 [1280], replicated, may hold values from 0.25 to 1.75
- window_ids: int32 [262144], P(('pipe', 'tensor')), may hold values from 0 to 127, as said below
- image_patches: int32 [2048], P(('pipe', 'tensor')), may hold values from 0 to 512, as said below
- image_sample: int32 [2048], P(('pipe', 'tensor')), may hold values from 0 to 7
Outputs:
- vision_seq: bfloat16 [16, 128, 32, 5120], P('pipe', None, 'tensor')
Inputs may be any that keep to these rules, and one draw needn't show every extreme that they name: `window_ids`: Non-decreasing within each bundle and equal over each 4 consecutive slots; every window lies within one aligned block of 64 slots of a bundle. `image_patches`: multiples of 128; the images of one bundle take at most 512 slots and at least half of them, and in every micro-batch some bundle is full.
All inputs are finite; a program needn't handle non-finite values.
Results may differ from a plain program's by a relative error of at most 0.0053.
Values may be sent and summed in bfloat16 or wider, within the bound.
No kernel may reach another device: no remote copies, remote signals or barrier semaphores. Data moves between devices by JAX's collectives and lax.ppermute only.
A program may use at most 64 MiB of HBM per device.

v0:
```python
import math
import jax
import jax.numpy as jnp
from jax import lax
from jax.sharding import PartitionSpec as P

HEADS = 16
WINDOW = 64
SAMPLES = 8
epsilon = 1e-06


def joined_along(blocks, dim):
    dims = list(blocks.shape[1:])
    dims[dim] *= blocks.shape[0]
    return jnp.moveaxis(blocks, 0, dim).reshape(dims)


def copy_for_each(x, axis):
    size = lax.axis_size(axis)
    return lax.all_to_all(jnp.broadcast_to(x[None], (size, *x.shape)), axis, 0, 0, tiled=True)


def gather_directly(x, axis, dim):
    return joined_along(copy_for_each(x, axis), dim)


def normalize(values, gain_row):
    return (
        values * lax.rsqrt(jnp.mean(values * values, axis=-1, keepdims=True) + epsilon) * gain_row
    )


def token_positions(starts, merged_count, token_count):
    offsets = jnp.cumsum(merged_count) - merged_count
    token_index = jnp.arange(token_count, dtype=jnp.int32)
    inside = (token_index[None, :] >= offsets[:, None]) & (
        token_index[None, :] < (offsets + merged_count)[:, None]
    )
    position = jnp.sum(
        jnp.where(inside, starts[:, None] + token_index[None, :] - offsets[:, None], 0), axis=0
    )
    return jnp.where(jnp.any(inside, axis=0), position, -1)


def body(patches, attn_gain, w_qkv, w_out, merge_gain, window_ids, image_patches, image_sample):
    patch_count, feature_width = patches.shape
    token_count = patch_count // 4
    group_size = lax.axis_size("tensor")
    own_index = lax.axis_index("tensor")
    residual = patches.astype(jnp.float32)
    normed = normalize(residual, attn_gain).astype(jnp.bfloat16)
    qkv_rows = gather_directly(w_qkv, "tensor", 0)
    qkv = jnp.dot(
        normed,
        lax.all_gather(qkv_rows, "pipe", axis=1, tiled=True),
        preferred_element_type=jnp.float32,
    ).astype(jnp.bfloat16)
    head_width = feature_width // HEADS
    tile_count = patch_count // WINDOW

    def split_heads(block):
        return block.reshape(tile_count, WINDOW, HEADS, head_width)

    queries = split_heads(qkv[:, :feature_width])
    keys_tile = split_heads(qkv[:, feature_width : 2 * feature_width])
    values_tile = split_heads(qkv[:, 2 * feature_width :])
    scores = jnp.einsum(
        "tqhd,tkhd->thqk", queries, keys_tile, preferred_element_type=jnp.float32
    ) * (1.0 / math.sqrt(head_width))
    live_row = jnp.arange(patch_count, dtype=jnp.int32) < jnp.sum(image_patches)
    window_tile = window_ids.reshape(tile_count, WINDOW)
    live_tile = live_row.reshape(tile_count, WINDOW)
    allowed = (window_tile[:, :, None] == window_tile[:, None, :]) & live_tile[:, None, :]
    scores = jnp.where(allowed[:, None, :, :], scores, -1e30)
    row_max = jnp.max(scores, axis=-1, keepdims=True)
    exponent = jnp.exp(scores - row_max)
    weights = (exponent / jnp.sum(exponent, axis=-1, keepdims=True)).astype(jnp.bfloat16)
    context = jnp.einsum(
        "thqk,tkhd->tqhd", weights, values_tile, preferred_element_type=jnp.float32
    ).reshape(patch_count, feature_width)
    context = jnp.where(live_row[:, None], context, 0.0).astype(jnp.bfloat16)
    proj_rows = lax.all_gather(w_out, "tensor", axis=0, tiled=True)
    attended = jnp.dot(
        context,
        lax.all_gather(proj_rows, "pipe", axis=1, tiled=True),
        preferred_element_type=jnp.float32,
    )
    hidden = residual + attended
    merged = (
        normalize(hidden, merge_gain).astype(jnp.bfloat16).reshape(token_count, 4 * feature_width)
    )
    outgoing = merged.reshape(token_count // group_size, group_size, 4 * feature_width)
    merged_count = image_patches // 4
    sample_hot = image_sample[:, None] == jnp.arange(SAMPLES, dtype=jnp.int32)[None, :]
    sample_tally = jnp.sum(jnp.where(sample_hot, merged_count[:, None], 0), axis=0)
    all_tallies = gather_directly(sample_tally[None, :], "tensor", 0)
    source_ranks = jnp.arange(group_size, dtype=jnp.int32)
    before = jnp.sum(jnp.where((source_ranks < own_index)[:, None], all_tallies, 0), axis=0)
    totals = jnp.sum(all_tallies, axis=0)
    sample_index = jnp.arange(SAMPLES, dtype=jnp.int32)
    sample_base = jnp.sum(
        jnp.where(sample_index[None, :] < sample_index[:, None], totals[None, :], 0), axis=1
    )
    image_order = jnp.arange(image_sample.shape[0], dtype=jnp.int32)
    same_before = (image_sample[None, :] == image_sample[:, None]) & (
        image_order[None, :] < image_order[:, None]
    )
    earlier = jnp.sum(jnp.where(same_before, merged_count[None, :], 0), axis=1)
    starts = jnp.sum(jnp.where(sample_hot, (sample_base + before)[None, :], 0), axis=1) + earlier
    position = token_positions(starts, merged_count, token_count)
    outgoing_position = position.reshape(token_count // group_size, group_size)
    received, received_position = (
        lax.all_to_all(outgoing, "tensor", split_axis=1, concat_axis=0, tiled=True),
        lax.all_to_all(outgoing_position, "tensor", split_axis=1, concat_axis=0, tiled=True),
    )
    dest_rows = received_position.reshape(token_count) // group_size
    placement = (jnp.arange(token_count, dtype=jnp.int32)[:, None] == dest_rows[None, :]).astype(
        jnp.bfloat16
    )
    placed = jnp.dot(
        placement,
        received.reshape(token_count, 4 * feature_width),
        preferred_element_type=jnp.float32,
    )
    return placed.astype(jnp.bfloat16).reshape(1, token_count, 1, 4 * feature_width)


def solution(mesh):
    return jax.shard_map(
        body,
        mesh=mesh,
        in_specs=(
            P(("pipe", "tensor"), None),
            P(),
            P("tensor", "pipe"),
            P("tensor", "pipe"),
            P(),
            P(("pipe", "tensor")),
            P(("pipe", "tensor")),
            P(("pipe", "tensor")),
        ),
        out_specs=P("pipe", None, "tensor", None),
        check_vma=False,
    )
```

profile of v0, /device:TPU:4, one launch (start us, length us, event | category | flops | bytes accessed | tf_op | source)
XLA Modules:
  0.0 208.7 jit_solution(4896109178755569658)
XLA Ops:
  6.6 0.9 broadcast_in_dim.144
  7.5 32.9 %all_to_all.38 = bf16[32,40,240]{2,1,0:T(8,128)(2,1)S(1)} all-to-all(bf16[32,40,240]{2,1,0:T(8,128)(2,1)S(1)} %broadcast_in_dim.144), channel_id=1, replica_groups=mesh['pipe'=16,'tensor'=32] {'tensor'}, dimensions={0} | all-to-all | bytes 1228800 | tf_op jit(solution)/shard_map/all_to_all | solution.py:21
  40.4 1.1 copy.60
  41.5 47.5 %all_gather.10 = bf16[1280,80]{1,0:T(8,128)(2,1)S(1)} all-gather(bf16[40,80]{1,0:T(8,128)(2,1)S(1)} %copy-done.3), channel_id=1, replica_groups=mesh['pipe'=16,'tensor'=32] {'tensor'}, dimensions={0}, use_global_device_ids=true | all-gather | bytes 211200 | tf_op jit(solution)/shard_map/all_gather | solution.py:83
  89.0 0.9 copy.66
  89.9 0.7 and_select_fusion.1
  90.7 0.6 broadcast_in_dim.96
  91.3 6.7 %all-to-all-start = ((s32[32,1,8]{2,1,0:T(1,128)}), s32[32,1,8]{2,1,0:T(1,128)S(1)}, u32[]{:S(2)}, u32[]{:S(2)}) async-start(s32[32,1,8]{2,1,0:T(1,128)} %broadcast_in_dim.96), calls=%async_computation | async-start | bytes 32768 | tf_op jit(solution)/shard_map/all_to_all | solution.py:21
  98.3 0.6 iota_compare_fusion.3
  98.9 0.6 add_compare_fusion
  99.8 0.3 fusion.3
  100.4 5.4 %all-to-all-done = s32[32,1,8]{2,1,0:T(1,128)S(1)} async-done(((s32[32,1,8]{2,1,0:T(1,128)}), s32[32,1,8]{2,1,0:T(1,128)S(1)}, u32[]{:S(2)}, u32[]{:S(2)}) %all-to-all-start) | async-done | bytes 1056 | tf_op jit(solution)/shard_map/all_to_all | solution.py:21
  106.4 0.7 copy.59
  107.1 5.7 %all-to-all-start.1 = ((s32[4,32,1]{0,2,1:T(1,128)}), s32[4,32,1]{0,2,1:T(1,128)S(1)}, u32[]{:S(2)}, u32[]{:S(2)}) async-start(s32[4,32,1]{0,2,1:T(1,128)} %copy.59), calls=%async_computation.1 | async-start | bytes 32768 | tf_op jit(solution)/shard_map/all_to_all | solution.py:115
  112.9 9.5 %convolution_convert_fusion.1 = bf16[512,3840]{1,0:T(8,128)(2,1)S(1)} fusion(bf16[1280,3840]{0,1:T(8,128)(2,1)} %all-gather.3.cloned.1.call-done, bf16[512,1280]{1,0:T(8,128)(2,1)S(1)} %copy-done.1, f32[1280]{0:T(1024)S(1)} %copy-done.7, f32[512]{0:T(512)S(1)} %add_rsqrt_fusion.1), kind=kOutput, calls=%fused_computation.2 | convolution fusion | flops 5037752320 | bytes 15080448 | tf_op jit(solution)/shard_map/dot_general | solution.py:54
  122.4 1.7 fusion.26
  124.1 4.1 %reshape.170 = bf16[8,64,16,80]{3,2,1,0:T(8,128)(2,1)S(1)} reshape(bf16[512,1280]{1,0:T(8,128)(2,1)} %get-tuple-element.7) | data formatting | bytes 2621440 | tf_op jit(solution)/shard_map/reshape | solution.py:63
  128.2 5.1 %reshape.171 = bf16[8,64,16,80]{3,2,1,0:T(8,128)(2,1)} reshape(bf16[512,1280]{1,0:T(8,128)(2,1)} %get-tuple-element.6) | data formatting | bytes 2621440 | tf_op jit(solution)/shard_map/reshape | solution.py:63
  133.3 4.1 %reshape.169 = bf16[8,64,16,80]{3,2,1,0:T(8,128)(2,1)} reshape(bf16[512,1280]{1,0:T(8,128)(2,1)S(1)} %get-tuple-element.5) | data formatting | bytes 2621440 | tf_op jit(solution)/shard_map/reshape | solution.py:63
  137.4 2.8 %fusion.7 = f32[8,16,64,64]{2,3,1,0:T(8,128)S(1)} fusion(bf16[8,64,16,80]{3,2,1,0:T(8,128)(2,1)} %reshape.171, bf16[8,64,16,80]{3,2,1,0:T(8,128)(2,1)S(1)} %reshape.170), kind=kOutput, calls=%fused_computation.19 | convolution fusion | flops 83886080 | bytes 4718592 | tf_op jit(solution)/shard_map/tqhd,tkhd->thqk/dot_general | solution.py:68
  140.2 1.5 fusion.27
  141.8 1.2 convolution_bitcast_fusion
  143.0 1.4 copy.65
  144.4 3.3 %reshape.172 = bf16[512,1280]{1,0:T(8,128)(2,1)} reshape(bf16[8,64,16,80]{3,2,1,0:T(8,128)(2,1)S(1)} %copy.65) | data formatting | bytes 2621440 | tf_op jit(solution)/shard_map/reshape | solution.py:81
  147.8 4.4 %multiply_reduce_fusion = (f32[512]{0:T(512)S(1)}, f32[512,1280]{1,0:T(8,128)S(1)}) fusion(bf16[1280,1280]{0,1:T(8,128)(2,1)} %all-gather.5.cloned.1.call-done, bf16[512,1280]{1,0:T(8,128)(2,1)} %reshape.172, pred[512]{0:T(512)(128)(4,1)S(1)} %iota_compare_fusion.3, bf16[512,1280]{1,0:T(8,128)(2,1)S(1)} %copy-done.2), kind=kOutput, calls=%fused_computation.15 | convolution fusion | flops 1680997888 | bytes 8522240 | tf_op jit(solution)/shard_map/dot_general | solution.py:84
  152.2 0.3 multiply_convert_fusion
  152.5 0.8 reshape_reshape.3
  153.3 2.1 copy.67
  155.4 10.5 %all-to-all-start.3 = ((bf16[4,32,5120]{2,0,1:T(4,128)(2,1)}), bf16[4,32,5120]{2,0,1:T(4,128)(2,1)S(1)}, u32[]{:S(2)}, u32[]{:S(2)}) async-start(bf16[4,32,5120]{2,0,1:T(4,128)(2,1)} %copy.67), calls=%async_computation.3 | async-start | bytes 2621440 | tf_op jit(solution)/shard_map/all_to_all | solution.py:114
  166.1 33.9 %all-to-all-done.3 = bf16[4,32,5120]{2,0,1:T(4,128)(2,1)S(1)} async-done(((bf16[4,32,5120]{2,0,1:T(4,128)(2,1)}), bf16[4,32,5120]{2,0,1:T(4,128)(2,1)S(1)}, u32[]{:S(2)}, u32[]{:S(2)}) %all-to-all-start.3) | async-done | bytes 1310752 | tf_op jit(solution)/shard_map/all_to_all | solution.py:114
  200.0 0.3 reshape.173
  200.3 1.6 fusion.1
  (47 shorter events, 2.1 us)
Async XLA Ops:
  6.5 35.0 %copy-start.3 = (bf16[40,80]{1,0:T(8,128)(2,1)S(1)}, bf16[40,80]{1,0:T(8,128)(2,1)}, u32[]{:S(2)}) copy-start(bf16[40,80]{1,0:T(8,128)(2,1)} %param.11) | copy-start | bytes 19204
  6.5 83.4 %copy-start.8 = (s32[4]{0:T(128)S(1)}, s32[4]{0:T(128)}, u32[]{:S(2)}) copy-start(s32[4]{0:T(128)} %param.14) | copy-start | bytes 52
  6.5 84.1 %copy-start.6 = (s32[4]{0:T(128)S(1)}, s32[4]{0:T(128)}, u32[]{:S(2)}) copy-start(s32[4]{0:T(128)} %param.15) | copy-start | bytes 52
  6.5 91.5 %copy-start.5 = (s32[512]{0:T(512)S(1)}, s32[512]{0:T(512)}, u32[]{:S(2)}) copy-start(s32[512]{0:T(512)} %param.13) | copy-start | bytes 6148
  6.5 93.3 %copy-start.1 = (bf16[512,1280]{1,0:T(8,128)(2,1)S(1)}, bf16[512,1280]{1,0:T(8,128)(2,1)}, u32[]{:S(2)}) copy-start(bf16[512,1280]{1,0:T(8,128)(2,1)} %param.8) | copy-start | bytes 3932164
  6.6 106.3 %all-gather.3.cloned.1.call-start = ((), (), s32[]{:S(2)}) async-start(), calls=%async_computation.4 | async-start | bytes 10444800 | tf_op jit(solution)/shard_map/all_gather | solution.py:56
  7.5 105.4 %copy-start.7 = (f32[1280]{0:T(1024)S(1)}, f32[1280]{0:T(1024)}, u32[]{:S(2)}) copy-start(f32[1280]{0:T(1024)} %param.9) | copy-start | bytes 15364
  41.4 106.4 %all-gather.5.cloned.1.call-start = ((), (), s32[]{:S(2)}) async-start(), calls=%async_computation.5 | async-start | bytes 3481600 | tf_op jit(solution)/shard_map/all_gather | solution.py:86
  91.3 14.5 %all-to-all-start = ((s32[32,1,8]{2,1,0:T(1,128)}), s32[32,1,8]{2,1,0:T(1,128)S(1)}, u32[]{:S(2)}, u32[]{:S(2)}) async-start(s32[32,1,8]{2,1,0:T(1,128)} %broadcast_in_dim.96), calls=%async_computation | async-start | bytes 32768 | tf_op jit(solution)/shard_map/all_to_all | solution.py:21
  107.1 48.3 %all-to-all-start.1 = ((s32[4,32,1]{0,2,1:T(1,128)}), s32[4,32,1]{0,2,1:T(1,128)S(1)}, u32[]{:S(2)}, u32[]{:S(2)}) async-start(s32[4,32,1]{0,2,1:T(1,128)} %copy.59), calls=%async_computation.1 | async-start | bytes 32768 | tf_op jit(solution)/shard_map/all_to_all | solution.py:115
  140.2 1.6 copy-start
  144.4 3.5 %copy-start.2 = (bf16[512,1280]{1,0:T(8,128)(2,1)S(1)}, bf16[512,1280]{1,0:T(8,128)(2,1)}, u32[]{:S(2)}) copy-start(bf16[512,1280]{1,0:T(8,128)(2,1)} %param.8) | copy-start | bytes 3932164
  147.6 4.5 %copy-start.4 = (f32[1280]{0:T(1024)S(1)}, f32[1280]{0:T(1024)}, u32[]{:S(2)}) copy-start(f32[1280]{0:T(1024)} %param.12) | copy-start | bytes 15364
  155.4 44.6 %all-to-all-start.3 = ((bf16[4,32,5120]{2,0,1:T(4,128)(2,1)}), bf16[4,32,5120]{2,0,1:T(4,128)(2,1)S(1)}, u32[]{:S(2)}, u32[]{:S(2)}) async-start(bf16[4,32,5120]{2,0,1:T(4,128)(2,1)} %copy.67), calls=%async_computation.3 | async-start | bytes 2621440 | tf_op jit(solution)/shard_map/all_to_all | solution.py:114
Sparse Core Ops, SparseCore 0:
  41.6 61.6 all-gather.2
  105.4 42.3 all-gather.4
where the time goes:
time: 209 us
  blocking collectives  80.4 us (38%)
  waiting for transfers between devices  39.5 us (19%)
  local copies, waits for them, and re-layouts  27.4 us (13%)
  starting transfers between devices  23 us (11%)
  matrix products  19.4 us (9%)
  between operations  13.6 us (7%)
  other arithmetic  5.39 us (3%)
    all_gather x1, blocking collectives, body(): proj_rows = lax.all_gather(w_out, 'tensor', axis=0, tiled=True)  47.5 us
    all_to_all x1, waiting for transfers between devices, body(): lax.all_to_all(outgoing, 'tensor', split_axis=1, concat_axis=0, tiled=True)  33.9 us
    all_to_all x1, blocking collectives, copy_for_each(): lax.all_to_all(jnp.broadcast_to(x[None], (size, *x.shape)), axis, 0, 0, t...  32.9 us
    reshape x3, local copies, waits for them, and re-layouts, split_heads(): return block.reshape(tile_count, WINDOW, HEADS, head_width)  13.2 us
    all_to_all x1, starting transfers between devices, body(): lax.all_to_all(outgoing, 'tensor', split_axis=1, concat_axis=0, tiled=True)  10.5 us
    dot_general x1, matrix products, body(): jnp.dot(normed, lax.all_gather(qkv_rows, 'pipe', axis=1, tiled=True), pre...  9.5 us
    all_to_all x1, starting transfers between devices, copy_for_each(): lax.all_to_all(jnp.broadcast_to(x[None], (size, *x.shape)), axis, 0, 0, t...  6.7 us
    all_to_all x1, starting transfers between devices, body(): lax.all_to_all(outgoing_position, 'tensor', split_axis=1, concat_axis=0,...  5.71 us
  transfers between devices with their start and end apart: 5, of which 3 were waited for; matrix products, arithmetic and copies ran while one was open for 23% of the time, Pallas kernels for 0%

commit v1 on v0

--- a/solution.py
+++ b/solution.py
@@ -8,6 +8,28 @@
 WINDOW = 64
 SAMPLES = 8
 epsilon = 1e-06
+
+
+def scan_slabs_by_axis(z, comm_axis):
+    response = lax.axis_size(comm_axis)
+    opened, f_now, answer = (response, lax.axis_index(comm_axis), z.shape[1])
+    by_place = [(dev_i, (dev_i + 1) % opened) for dev_i in range(opened)]
+    copies = [(dev_i, (dev_i - 1) % opened) for dev_i in range(opened)]
+    reached = jnp.zeros((*z.shape[:1], opened * answer, *z.shape[2:]), z.dtype)
+    reached = lax.dynamic_update_slice_in_dim(reached, z, f_now * answer, axis=1)
+    taken_in = local_out = z
+    shaped = opened // 2
+    for pp in range(1, shaped + 1):
+        taken_in = lax.ppermute(taken_in, comm_axis, by_place)
+        reached = lax.dynamic_update_slice_in_dim(
+            reached, taken_in, (f_now - pp) % opened * answer, axis=1
+        )
+        if pp < opened - shaped:
+            local_out = lax.ppermute(local_out, comm_axis, copies)
+            reached = lax.dynamic_update_slice_in_dim(
+                reached, local_out, (f_now + pp) % opened * answer, axis=1
+            )
+    return reached
 
 
 def joined_along(blocks, dim):
@@ -82,9 +104,7 @@
     context = jnp.where(live_row[:, None], context, 0.0).astype(jnp.bfloat16)
     proj_rows = lax.all_gather(w_out, "tensor", axis=0, tiled=True)
     attended = jnp.dot(
-        context,
-        lax.all_gather(proj_rows, "pipe", axis=1, tiled=True),
-        preferred_element_type=jnp.float32,
+        context, scan_slabs_by_axis(proj_rows, "pipe"), preferred_element_type=jnp.float32
     )
     hidden = residual + attended
     merged = (

time: 209 us -> 332 us (1.59)
  the two profiles are of different devices: /device:TPU:4 before, /device:TPU:29 now
where the time goes in v1:
time: 332 us; the launch traced here: 329 us
  local copies, waits for them, and re-layouts  105 us (32%)
  blocking collectives  69.9 us (21%)
  starting transfers between devices  61 us (18%)
  waiting for transfers between devices  54 us (16%)
  matrix products  19.6 us (6%)
  between operations  13.9 us (4%)
  other arithmetic  5.4 us (2%)
    all_gather x1, blocking collectives, body(): proj_rows = lax.all_gather(w_out, 'tensor', axis=0, tiled=True)  38.8 us
    dynamic_update_slice x8, local copies, waits for them, and re-layouts, scan_slabs_by_axis(): lax.dynamic_update_slice_in_dim(reached, taken_in, (f_now - pp) % opened...  38 us
    ppermute x8, starting transfers between devices, scan_slabs_by_axis(): taken_in = lax.ppermute(taken_in, comm_axis, by_place)  37.2 us
    dynamic_update_slice x7, local copies, waits for them, and re-layouts, scan_slabs_by_axis(): lax.dynamic_update_slice_in_dim(reached, local_out, (f_now + pp) % opened...  33.4 us
    all_to_all x1, waiting for transfers between devices, body(): lax.all_to_all(outgoing, 'tensor', split_axis=1, concat_axis=0, tiled=True)  32.9 us
    all_to_all x1, blocking collectives, copy_for_each(): lax.all_to_all(jnp.broadcast_to(x[None], (size, *x.shape)), axis, 0, 0, t...  31.1 us
    reshape x3, local copies, waits for them, and re-layouts, split_heads(): return block.reshape(tile_count, WINDOW, HEADS, head_width)  13.2 us
    ppermute x8, waiting for transfers between devices, scan_slabs_by_axis(): taken_in = lax.ppermute(taken_in, comm_axis, by_place)  10.6 us
  transfers between devices with their start and end apart: 19, of which 9 were waited for; matrix products, arithmetic and copies ran while one was open for 38% of the time, Pallas kernels for 0%

profile of v1, /device:TPU:29, one launch (start us, length us, event | category | flops | bytes accessed | tf_op | source)
XLA Modules:
  0.0 329.3 jit_solution(11268163681671128562)
XLA Ops:
  7.5 31.1 %all_to_all.38 = bf16[32,40,240]{2,1,0:T(8,128)(2,1)S(1)} all-to-all(bf16[32,40,240]{2,1,0:T(8,128)(2,1)S(1)} %broadcast_in_dim.147), channel_id=1, replica_groups=mesh['pipe'=16,'tensor'=32] {'tensor'}, dimensions={0} | all-to-all | bytes 1228800 | tf_op jit(solution)/shard_map/all_to_all | solution.py:43
  39.7 38.8 %all_gather.7 = bf16[1280,80]{1,0:T(8,128)(2,1)S(1)} all-gather(bf16[40,80]{1,0:T(8,128)(2,1)S(1)} %copy-done.12), channel_id=1, replica_groups=mesh['pipe'=16,'tensor'=32] {'tensor'}, dimensions={0}, use_global_device_ids=true | all-gather | bytes 211200 | tf_op jit(solution)/shard_map/all_gather | solution.py:105
  78.5 13.5 %collective-permute-start = (bf16[1280,80]{1,0:T(8,128)(2,1)S(1)}, bf16[1280,80]{1,0:T(8,128)(2,1)S(1)}, u32[]{:S(2)}, u32[]{:S(2)}) collective-permute-start(bf16[1280,80]{1,0:T(8,128)(2,1)S(1)} %all_gather.7), channel_id=1, source_target_pairs={{0,32},{32,64},{64,96},{96,128},{128,160},{160,192},{192,224},{224... | collective-permute-start | bytes 614408 | tf_op jit(solution)/shard_map/ppermute | solution.py:23
  93.3 6.4 %all-to-all-start = ((s32[32,1,8]{2,1,0:T(1,128)}), s32[32,1,8]{2,1,0:T(1,128)S(1)}, u32[]{:S(2)}, u32[]{:S(2)}) async-start(s32[32,1,8]{2,1,0:T(1,128)} %broadcast_in_dim.136), calls=%async_computation | async-start | bytes 32768 | tf_op jit(solution)/shard_map/all_to_all | solution.py:43
  101.8 3.7 %collective-permute-start.2 = (bf16[1280,80]{1,0:T(8,128)(2,1)S(1)}, bf16[1280,80]{1,0:T(8,128)(2,1)S(1)}, u32[]{:S(2)}, u32[]{:S(2)}) collective-permute-start(bf16[1280,80]{1,0:T(8,128)(2,1)S(1)} %collective-permute-done), channel_id=1, source_target_pairs={{0,32},{32,64},{64,96},{96,128},{128,160},{160,192},{192,224},{224... | collective-permute-start | bytes 614408 | tf_op jit(solution)/shard_map/ppermute | solution.py:23
  124.9 3.8 %collective-permute-start.8 = (bf16[1280,80]{1,0:T(8,128)(2,1)}, bf16[1280,80]{1,0:T(8,128)(2,1)}, u32[]{:S(2)}, u32[]{:S(2)}) collective-permute-start(bf16[1280,80]{1,0:T(8,128)(2,1)} %collective-permute-done.6), channel_id=1, source_target_pairs={{0,32},{32,64},{64,96},{96,128},{128,160},{160,192},{192,224},{224... | collective-permute-start | bytes 614408 | tf_op jit(solution)/shard_map/ppermute | solution.py:23
  129.0 4.9 %dynamic_update_slice.48 = bf16[1280,1280]{1,0:T(8,128)(2,1)S(1)} dynamic-update-slice(bf16[1280,1280]{1,0:T(8,128)(2,1)S(1)} %broadcast_in_dim.151, bf16[1280,80]{1,0:T(8,128)(2,1)} %copy-done.4, s32[]{:T(128)} %constant.130.clone.1, s32[]{:T(128)S(6)} %select_n.184) | dynamic-update-slice | bytes 409604 | tf_op jit(solution)/shard_map/dynamic_update_slice | solution.py:19
  137.2 4.7 %collective-permute-done.9 = bf16[1280,80]{1,0:T(8,128)(2,1)S(1)} collective-permute-done((bf16[1280,80]{1,0:T(8,128)(2,1)}, bf16[1280,80]{1,0:T(8,128)(2,1)S(1)}, u32[]{:S(2)}, u32[]{:S(2)}) %collective-permute-start.9) | collective-permute-done | bytes 204832 | tf_op jit(solution)/shard_map/ppermute | solution.py:28
  145.9 4.6 %collective-permute-done.11 = bf16[1280,80]{1,0:T(8,128)(2,1)} collective-permute-done((bf16[1280,80]{1,0:T(8,128)(2,1)S(1)}, bf16[1280,80]{1,0:T(8,128)(2,1)}, u32[]{:S(2)}, u32[]{:S(2)}) %collective-permute-start.11) | collective-permute-done | bytes 204832 | tf_op jit(solution)/shard_map/ppermute | solution.py:28
  154.3 8.1 %all-to-all-start.1 = ((s32[4,32,1]{0,2,1:T(1,128)}), s32[4,32,1]{0,2,1:T(1,128)S(1)}, u32[]{:S(2)}, u32[]{:S(2)}) async-start(s32[4,32,1]{0,2,1:T(1,128)} %copy.47), calls=%async_computation.1 | async-start | bytes 32768 | tf_op jit(solution)/shard_map/all_to_all | solution.py:135
  162.4 4.9 %dynamic_update_slice.49 = bf16[1280,1280]{1,0:T(8,128)(2,1)S(1)} dynamic-update-slice(bf16[1280,1280]{1,0:T(8,128)(2,1)S(1)} %dynamic_update_slice.48, bf16[1280,80]{1,0:T(8,128)(2,1)} %copy-done.5, s32[]{:T(128)} %constant.130.clone.1, s32[]{:T(128)S(6)} %select_n.186) | dynamic-update-slice | bytes 409604 | tf_op jit(solution)/shard_map/dynamic_update_slice | solution.py:24
  167.3 4.1 %dynamic_update_slice.50 = bf16[1280,1280]{1,0:T(8,128)(2,1)S(1)} dynamic-update-slice(bf16[1280,1280]{1,0:T(8,128)(2,1)S(1)} %dynamic_update_slice.49, bf16[1280,80]{1,0:T(8,128)(2,1)} %copy-done.6, s32[]{:T(128)} %constant.130.clone.1, s32[]{:T(128)S(6)} %select_n.188) | dynamic-update-slice | bytes 409604 | tf_op jit(solution)/shard_map/dynamic_update_slice | solution.py:29
  171.3 4.9 %dynamic_update_slice.51 = bf16[1280,1280]{1,0:T(8,128)(2,1)S(1)} dynamic-update-slice(bf16[1280,1280]{1,0:T(8,128)(2,1)S(1)} %dynamic_update_slice.50, bf16[1280,80]{1,0:T(8,128)(2,1)} %copy-done.7, s32[]{:T(128)} %constant.130.clone.1, s32[]{:T(128)S(6)} %select_n.190) | dynamic-update-slice | bytes 409604 | tf_op jit(solution)/shard_map/dynamic_update_slice | solution.py:24
  176.2 4.9 %dynamic_update_slice.52 = bf16[1280,1280]{1,0:T(8,128)(2,1)S(1)} dynamic-update-slice(bf16[1280,1280]{1,0:T(8,128)(2,1)S(1)} %dynamic_update_slice.51, bf16[1280,80]{1,0:T(8,128)(2,1)} %copy-done.8, s32[]{:T(128)} %constant.130.clone.1, s32[]{:T(128)S(6)} %select_n.192) | dynamic-update-slice | bytes 409604 | tf_op jit(solution)/shard_map/dynamic_update_slice | solution.py:29
  181.1 4.9 %dynamic_update_slice.53 = bf16[1280,1280]{1,0:T(8,128)(2,1)S(1)} dynamic-update-slice(bf16[1280,1280]{1,0:T(8,128)(2,1)S(1)} %dynamic_update_slice.52, bf16[1280,80]{1,0:T(8,128)(2,1)} %copy-done.9, s32[]{:T(128)} %constant.130.clone.1, s32[]{:T(128)S(6)} %select_n.194) | dynamic-update-slice | bytes 409604 | tf_op jit(solution)/shard_map/dynamic_update_slice | solution.py:24
  186.0 4.9 %dynamic_update_slice.54 = bf16[1280,1280]{1,0:T(8,128)(2,1)S(1)} dynamic-update-slice(bf16[1280,1280]{1,0:T(8,128)(2,1)S(1)} %dynamic_update_slice.53, bf16[1280,80]{1,0:T(8,128)(2,1)} %collective-permute-done.5, s32[]{:T(128)} %constant.130.clone.1, s32[]{:T(128)S(6)} %select_n.196) | dynamic-update-slice | bytes 409604 | tf_op jit(solution)/shard_map/dynamic_update_slice | solution.py:29
  190.9 4.9 %dynamic_update_slice.55 = bf16[1280,1280]{1,0:T(8,128)(2,1)S(1)} dynamic-update-slice(bf16[1280,1280]{1,0:T(8,128)(2,1)S(1)} %dynamic_update_slice.54, bf16[1280,80]{1,0:T(8,128)(2,1)} %collective-permute-done.6, s32[]{:T(128)} %constant.130.clone.1, s32[]{:T(128)S(6)} %select_n.198) | dynamic-update-slice | bytes 409604 | tf_op jit(solution)/shard_map/dynamic_update_slice | solution.py:24
  195.8 4.9 %dynamic_update_slice.56 = bf16[1280,1280]{1,0:T(8,128)(2,1)S(1)} dynamic-update-slice(bf16[1280,1280]{1,0:T(8,128)(2,1)S(1)} %dynamic_update_slice.55, bf16[1280,80]{1,0:T(8,128)(2,1)} %collective-permute-done.7, s32[]{:T(128)} %constant.130.clone.1, s32[]{:T(128)S(6)} %select_n.200) | dynamic-update-slice | bytes 409604 | tf_op jit(solution)/shard_map/dynamic_update_slice | solution.py:29
  200.7 4.9 %dynamic_update_slice.57 = bf16[1280,1280]{1,0:T(8,128)(2,1)S(1)} dynamic-update-slice(bf16[1280,1280]{1,0:T(8,128)(2,1)S(1)} %dynamic_update_slice.56, bf16[1280,80]{1,0:T(8,128)(2,1)} %collective-permute-done.8, s32[]{:T(128)} %constant.130.clone.1, s32[]{:T(128)S(6)} %select_n.202) | dynamic-update-slice | bytes 409604 | tf_op jit(solution)/shard_map/dynamic_update_slice | solution.py:24
  205.6 4.9 %dynamic_update_slice.58 = bf16[1280,1280]{1,0:T(8,128)(2,1)S(1)} dynamic-update-slice(bf16[1280,1280]{1,0:T(8,128)(2,1)S(1)} %dynamic_update_slice.57, bf16[1280,80]{1,0:T(8,128)(2,1)} %copy-done.10, s32[]{:T(128)} %constant.130.clone.1, s32[]{:T(128)S(6)} %select_n.204) | dynamic-update-slice | bytes 409604 | tf_op jit(solution)/shard_map/dynamic_update_slice | solution.py:29
  210.5 4.9 %dynamic_update_slice.59 = bf16[1280,1280]{1,0:T(8,128)(2,1)S(1)} dynamic-update-slice(bf16[1280,1280]{1,0:T(8,128)(2,1)S(1)} %dynamic_update_slice.58, bf16[1280,80]{1,0:T(8,128)(2,1)} %copy-done.11, s32[]{:T(128)} %constant.130.clone.1, s32[]{:T(128)S(6)} %select_n.206) | dynamic-update-slice | bytes 409604 | tf_op jit(solution)/shard_map/dynamic_update_slice | solution.py:24
  215.4 4.9 %dynamic_update_slice.60 = bf16[1280,1280]{1,0:T(8,128)(2,1)S(1)} dynamic-update-slice(bf16[1280,1280]{1,0:T(8,128)(2,1)S(1)} %dynamic_update_slice.59, bf16[1280,80]{1,0:T(8,128)(2,1)} %collective-permute-done.11, s32[]{:T(128)} %constant.130.clone.1, s32[]{:T(128)S(6)} %select_n.208) | dynamic-update-slice | bytes 409604 | tf_op jit(solution)/shard_map/dynamic_update_slice | solution.py:29
  220.3 4.1 %dynamic_update_slice.61 = bf16[1280,1280]{1,0:T(8,128)(2,1)S(1)} dynamic-update-slice(bf16[1280,1280]{1,0:T(8,128)(2,1)S(1)} %dynamic_update_slice.60, bf16[1280,80]{1,0:T(8,128)(2,1)} %collective-permute-done.12, s32[]{:T(128)} %constant.130.clone.1, s32[]{:T(128)S(6)} %select_n.210) | dynamic-update-slice | bytes 409604 | tf_op jit(solution)/shard_map/dynamic_update_slice | solution.py:24
  224.4 4.9 %dynamic_update_slice.62 = bf16[1280,1280]{1,0:T(8,128)(2,1)S(1)} dynamic-update-slice(bf16[1280,1280]{1,0:T(8,128)(2,1)S(1)} %dynamic_update_slice.61, bf16[1280,80]{1,0:T(8,128)(2,1)} %collective-permute-done.13, s32[]{:T(128)} %constant.130.clone.1, s32[]{:T(128)S(6)} %select_n.212) | dynamic-update-slice | bytes 409604 | tf_op jit(solution)/shard_map/dynamic_update_slice | solution.py:29
  229.3 4.6 %dynamic_update_slice.63 = bf16[1280,1280]{1,0:T(8,128)(2,1)S(1)} dynamic-update-slice(bf16[1280,1280]{1,0:T(8,128)(2,1)S(1)} %dynamic_update_slice.62, bf16[1280,80]{1,0:T(8,128)(2,1)} %collective-permute-done.14, s32[]{:T(128)} %constant.130.clone.1, s32[]{:T(128)S(6)} %select_n.214) | dynamic-update-slice | bytes 409604 | tf_op jit(solution)/shard_map/dynamic_update_slice | solution.py:24
  235.7 9.7 %convolution_convert_fusion.1 = bf16[512,3840]{1,0:T(8,128)(2,1)S(1)} fusion(bf16[1280,3840]{0,1:T(8,128)(2,1)} %all-gather.2.cloned.1.call-done, bf16[512,1280]{1,0:T(8,128)(2,1)} %param.8, f32[1280]{0:T(1024)S(1)} %copy-done.16, f32[512]{0:T(512)S(1)} %add_rsqrt_fusion.1), kind=kOutput, calls=%fused_computation.2 | convolution fusion | flops 5037752320 | bytes 15080448 | tf_op jit(solution)/shard_map/dot_general | solution.py:76
  247.1 4.1 %reshape.170 = bf16[8,64,16,80]{3,2,1,0:T(8,128)(2,1)S(1)} reshape(bf16[512,1280]{1,0:T(8,128)(2,1)} %get-tuple-element.7) | data formatting | bytes 2621440 | tf_op jit(solution)/shard_map/reshape | solution.py:85
  251.2 5.0 %reshape.171 = bf16[8,64,16,80]{3,2,1,0:T(8,128)(2,1)} reshape(bf16[512,1280]{1,0:T(8,128)(2,1)} %get-tuple-element.6) | data formatting | bytes 2621440 | tf_op jit(solution)/shard_map/reshape | solution.py:85
  256.3 4.1 %reshape.169 = bf16[8,64,16,80]{3,2,1,0:T(8,128)(2,1)} reshape(bf16[512,1280]{1,0:T(8,128)(2,1)S(1)} %get-tuple-element.5) | data formatting | bytes 2621440 | tf_op jit(solution)/shard_map/reshape | solution.py:85
  270.6 4.4 %multiply_reduce_fusion = (f32[512]{0:T(512)S(1)}, f32[512,1280]{1,0:T(8,128)S(1)}) fusion(bf16[1280,1280]{1,0:T(8,128)(2,1)} %copy-done, bf16[512,1280]{1,0:T(8,128)(2,1)} %reshape.172, pred[512]{0:T(512)(128)(4,1)S(1)} %iota_compare_fusion.3, bf16[512,1280]{1,0:T(8,128)(2,1)S(1)} %copy-done.3), kind=kOutput, calls=%fused_computation.15 | convolution fusion | flops 1680997888 | bytes 8522240 | tf_op jit(solution)/shard_map/dot_general | solution.py:106
  278.2 9.2 %all-to-all-start.3 = ((bf16[4,32,5120]{2,0,1:T(4,128)(2,1)}), bf16[4,32,5120]{2,0,1:T(4,128)(2,1)S(1)}, u32[]{:S(2)}, u32[]{:S(2)}) async-start(bf16[4,32,5120]{2,0,1:T(4,128)(2,1)} %copy.54), calls=%async_computation.3 | async-start | bytes 2621440 | tf_op jit(solution)/shard_map/all_to_all | solution.py:134
  287.6 32.9 %all-to-all-done.3 = bf16[4,32,5120]{2,0,1:T(4,128)(2,1)S(1)} async-done(((bf16[4,32,5120]{2,0,1:T(4,128)(2,1)}), bf16[4,32,5120]{2,0,1:T(4,128)(2,1)S(1)}, u32[]{:S(2)}, u32[]{:S(2)}) %all-to-all-start.3) | async-done | bytes 1310752 | tf_op jit(solution)/shard_map/all_to_all | solution.py:134
  (108 shorter events, 54.9 us)
Async XLA Ops:
  6.5 33.1 %copy-start.12 = (bf16[40,80]{1,0:T(8,128)(2,1)S(1)}, bf16[40,80]{1,0:T(8,128)(2,1)}, u32[]{:S(2)}) copy-start(bf16[40,80]{1,0:T(8,128)(2,1)} %param.11) | copy-start | bytes 19204
  6.5 85.4 %copy-start.17 = (s32[4]{0:T(128)S(1)}, s32[4]{0:T(128)}, u32[]{:S(2)}) copy-start(s32[4]{0:T(128)} %param.14) | copy-start | bytes 52
  6.5 86.1 %copy-start.15 = (s32[4]{0:T(128)S(1)}, s32[4]{0:T(128)}, u32[]{:S(2)}) copy-start(s32[4]{0:T(128)} %param.15) | copy-start | bytes 52
  6.5 93.2 %copy-start.14 = (s32[512]{0:T(512)S(1)}, s32[512]{0:T(512)}, u32[]{:S(2)}) copy-start(s32[512]{0:T(512)} %param.13) | copy-start | bytes 6148
  6.5 114.4 %copy-start.2 = (bf16[512,1280]{1,0:T(8,128)(2,1)S(1)}, bf16[512,1280]{1,0:T(8,128)(2,1)}, u32[]{:S(2)}) copy-start(bf16[512,1280]{1,0:T(8,128)(2,1)} %param.8) | copy-start | bytes 3932164
  6.6 227.4 %all-gather.2.cloned.1.call-start = ((), (), s32[]{:S(2)}) async-start(), calls=%async_computation.4 | async-start | bytes 10444800 | tf_op jit(solution)/shard_map/all_gather | solution.py:78
  78.4 50.3 %copy-start.4 = (bf16[1280,80]{1,0:T(8,128)(2,1)}, bf16[1280,80]{1,0:T(8,128)(2,1)S(1)}, u32[]{:S(2)}) copy-start(bf16[1280,80]{1,0:T(8,128)(2,1)S(1)} %all_gather.7) | copy-start | bytes 614404
  78.5 23.3 %collective-permute-start = (bf16[1280,80]{1,0:T(8,128)(2,1)S(1)}, bf16[1280,80]{1,0:T(8,128)(2,1)S(1)}, u32[]{:S(2)}, u32[]{:S(2)}) collective-permute-start(bf16[1280,80]{1,0:T(8,128)(2,1)S(1)} %all_gather.7), channel_id=1, source_target_pairs={{0,32},{32,64},{64,96},{96,128},{128,160},{160,192},{192,224},{224... | collective-permute-start | bytes 614408 | tf_op jit(solution)/shard_map/ppermute | solution.py:23
  91.9 14.3 %collective-permute-start.1 = (bf16[1280,80]{1,0:T(8,128)(2,1)S(1)}, bf16[1280,80]{1,0:T(8,128)(2,1)S(1)}, u32[]{:S(2)}, u32[]{:S(2)}) collective-permute-start(bf16[1280,80]{1,0:T(8,128)(2,1)S(1)} %all_gather.7), channel_id=1, source_target_pairs={{0,480},{32,0},{64,32},{96,64},{128,96},{160,128},{192,160},{224,1... | collective-permute-start | bytes 614408 | tf_op jit(solution)/shard_map/ppermute | solution.py:28
  93.3 40.6 %all-to-all-start = ((s32[32,1,8]{2,1,0:T(1,128)}), s32[32,1,8]{2,1,0:T(1,128)S(1)}, u32[]{:S(2)}, u32[]{:S(2)}) async-start(s32[32,1,8]{2,1,0:T(1,128)} %broadcast_in_dim.136), calls=%async_computation | async-start | bytes 32768 | tf_op jit(solution)/shard_map/all_to_all | solution.py:43
  101.8 26.9 %copy-start.5 = (bf16[1280,80]{1,0:T(8,128)(2,1)}, bf16[1280,80]{1,0:T(8,128)(2,1)S(1)}, u32[]{:S(2)}) copy-start(bf16[1280,80]{1,0:T(8,128)(2,1)S(1)} %collective-permute-done) | copy-start | bytes 614404
  101.8 7.7 %collective-permute-start.2 = (bf16[1280,80]{1,0:T(8,128)(2,1)S(1)}, bf16[1280,80]{1,0:T(8,128)(2,1)S(1)}, u32[]{:S(2)}, u32[]{:S(2)}) collective-permute-start(bf16[1280,80]{1,0:T(8,128)(2,1)S(1)} %collective-permute-done), channel_id=1, source_target_pairs={{0,32},{32,64},{64,96},{96,128},{128,160},{160,192},{192,224},{224... | collective-permute-start | bytes 614408 | tf_op jit(solution)/shard_map/ppermute | solution.py:23
  106.2 22.5 %copy-start.6 = (bf16[1280,80]{1,0:T(8,128)(2,1)}, bf16[1280,80]{1,0:T(8,128)(2,1)S(1)}, u32[]{:S(2)}) copy-start(bf16[1280,80]{1,0:T(8,128)(2,1)S(1)} %collective-permute-done.1) | copy-start | bytes 614404
  106.2 7.7 %collective-permute-start.3 = (bf16[1280,80]{1,0:T(8,128)(2,1)S(1)}, bf16[1280,80]{1,0:T(8,128)(2,1)S(1)}, u32[]{:S(2)}, u32[]{:S(2)}) collective-permute-start(bf16[1280,80]{1,0:T(8,128)(2,1)S(1)} %collective-permute-done.1), channel_id=1, source_target_pairs={{0,480},{32,0},{64,32},{96,64},{128,96},{160,128},{192,160},{224,1... | collective-permute-start | bytes 614408 | tf_op jit(solution)/shard_map/ppermute | solution.py:28
  109.5 4.5 %copy-start.7 = (bf16[1280,80]{1,0:T(8,128)(2,1)}, bf16[1280,80]{1,0:T(8,128)(2,1)S(1)}, u32[]{:S(2)}) copy-start(bf16[1280,80]{1,0:T(8,128)(2,1)S(1)} %collective-permute-done.2) | copy-start | bytes 614404
  109.5 7.7 %collective-permute-start.4 = (bf16[1280,80]{1,0:T(8,128)(2,1)S(1)}, bf16[1280,80]{1,0:T(8,128)(2,1)S(1)}, u32[]{:S(2)}, u32[]{:S(2)}) collective-permute-start(bf16[1280,80]{1,0:T(8,128)(2,1)S(1)} %collective-permute-done.2), channel_id=1, source_target_pairs={{0,32},{32,64},{64,96},{96,128},{128,160},{160,192},{192,224},{224... | collective-permute-start | bytes 614408 | tf_op jit(solution)/shard_map/ppermute | solution.py:23
  114.0 14.8 %copy-start.8 = (bf16[1280,80]{1,0:T(8,128)(2,1)}, bf16[1280,80]{1,0:T(8,128)(2,1)S(1)}, u32[]{:S(2)}) copy-start(bf16[1280,80]{1,0:T(8,128)(2,1)S(1)} %collective-permute-done.3) | copy-start | bytes 614404
  114.0 7.8 %collective-permute-start.5 = (bf16[1280,80]{1,0:T(8,128)(2,1)S(1)}, bf16[1280,80]{1,0:T(8,128)(2,1)}, u32[]{:S(2)}, u32[]{:S(2)}) collective-permute-start(bf16[1280,80]{1,0:T(8,128)(2,1)S(1)} %collective-permute-done.3), channel_id=1, source_target_pairs={{0,480},{32,0},{64,32},{96,64},{128,96},{160,128},{192,160},{224,1... | collective-permute-start | bytes 614408 | tf_op jit(solution)/shard_map/ppermute | solution.py:28
  117.2 11.5 %copy-start.9 = (bf16[1280,80]{1,0:T(8,128)(2,1)}, bf16[1280,80]{1,0:T(8,128)(2,1)S(1)}, u32[]{:S(2)}) copy-start(bf16[1280,80]{1,0:T(8,128)(2,1)S(1)} %collective-permute-done.4) | copy-start | bytes 614404
  117.2 7.7 %collective-permute-start.6 = (bf16[1280,80]{1,0:T(8,128)(2,1)S(1)}, bf16[1280,80]{1,0:T(8,128)(2,1)}, u32[]{:S(2)}, u32[]{:S(2)}) collective-permute-start(bf16[1280,80]{1,0:T(8,128)(2,1)S(1)} %collective-permute-done.4), channel_id=1, source_target_pairs={{0,32},{32,64},{64,96},{96,128},{128,160},{160,192},{192,224},{224... | collective-permute-start | bytes 614408 | tf_op jit(solution)/shard_map/ppermute | solution.py:23
  121.8 12.3 %collective-permute-start.7 = (bf16[1280,80]{1,0:T(8,128)(2,1)}, bf16[1280,80]{1,0:T(8,128)(2,1)}, u32[]{:S(2)}, u32[]{:S(2)}) collective-permute-start(bf16[1280,80]{1,0:T(8,128)(2,1)} %collective-permute-done.5), channel_id=1, source_target_pairs={{0,480},{32,0},{64,32},{96,64},{128,96},{160,128},{192,160},{224,1... | collective-permute-start | bytes 614408 | tf_op jit(solution)/shard_map/ppermute | solution.py:28
  124.9 9.1 %collective-permute-start.8 = (bf16[1280,80]{1,0:T(8,128)(2,1)}, bf16[1280,80]{1,0:T(8,128)(2,1)}, u32[]{:S(2)}, u32[]{:S(2)}) collective-permute-start(bf16[1280,80]{1,0:T(8,128)(2,1)} %collective-permute-done.6), channel_id=1, source_target_pairs={{0,32},{32,64},{64,96},{96,128},{128,160},{160,192},{192,224},{224... | collective-permute-start | bytes 614408 | tf_op jit(solution)/shard_map/ppermute | solution.py:23
  134.0 7.9 %collective-permute-start.9 = (bf16[1280,80]{1,0:T(8,128)(2,1)}, bf16[1280,80]{1,0:T(8,128)(2,1)S(1)}, u32[]{:S(2)}, u32[]{:S(2)}) collective-permute-start(bf16[1280,80]{1,0:T(8,128)(2,1)} %collective-permute-done.7), channel_id=1, source_target_pairs={{0,480},{32,0},{64,32},{96,64},{128,96},{160,128},{192,160},{224,1... | collective-permute-start | bytes 614408 | tf_op jit(solution)/shard_map/ppermute | solution.py:28
  134.1 8.6 %collective-permute-start.10 = (bf16[1280,80]{1,0:T(8,128)(2,1)}, bf16[1280,80]{1,0:T(8,128)(2,1)S(1)}, u32[]{:S(2)}, u32[]{:S(2)}) collective-permute-start(bf16[1280,80]{1,0:T(8,128)(2,1)} %collective-permute-done.8), channel_id=1, source_target_pairs={{0,32},{32,64},{64,96},{96,128},{128,160},{160,192},{192,224},{224... | collective-permute-start | bytes 614408 | tf_op jit(solution)/shard_map/ppermute | solution.py:23
  142.7 7.8 %collective-permute-start.11 = (bf16[1280,80]{1,0:T(8,128)(2,1)S(1)}, bf16[1280,80]{1,0:T(8,128)(2,1)}, u32[]{:S(2)}, u32[]{:S(2)}) collective-permute-start(bf16[1280,80]{1,0:T(8,128)(2,1)S(1)} %collective-permute-done.9), channel_id=1, source_target_pairs={{0,480},{32,0},{64,32},{96,64},{128,96},{160,128},{192,160},{224,1... | collective-permute-start | bytes 614408 | tf_op jit(solution)/shard_map/ppermute | solution.py:28
  142.7 7.8 %copy-start.11 = (bf16[1280,80]{1,0:T(8,128)(2,1)}, bf16[1280,80]{1,0:T(8,128)(2,1)S(1)}, u32[]{:S(2)}) copy-start(bf16[1280,80]{1,0:T(8,128)(2,1)S(1)} %collective-permute-done.10) | copy-start | bytes 614404
  142.7 7.8 %collective-permute-start.12 = (bf16[1280,80]{1,0:T(8,128)(2,1)S(1)}, bf16[1280,80]{1,0:T(8,128)(2,1)}, u32[]{:S(2)}, u32[]{:S(2)}) collective-permute-start(bf16[1280,80]{1,0:T(8,128)(2,1)S(1)} %collective-permute-done.10), channel_id=1, source_target_pairs={{0,32},{32,64},{64,96},{96,128},{128,160},{160,192},{192,224},{224... | collective-permute-start | bytes 614408 | tf_op jit(solution)/shard_map/ppermute | solution.py:23
  150.5 73.8 %collective-permute-start.13 = (bf16[1280,80]{1,0:T(8,128)(2,1)}, bf16[1280,80]{1,0:T(8,128)(2,1)}, u32[]{:S(2)}, u32[]{:S(2)}) collective-permute-start(bf16[1280,80]{1,0:T(8,128)(2,1)} %collective-permute-done.11), channel_id=1, source_target_pairs={{0,480},{32,0},{64,32},{96,64},{128,96},{160,128},{192,160},{224,1... | collective-permute-start | bytes 614408 | tf_op jit(solution)/shard_map/ppermute | solution.py:28
  150.5 78.7 %collective-permute-start.14 = (bf16[1280,80]{1,0:T(8,128)(2,1)}, bf16[1280,80]{1,0:T(8,128)(2,1)}, u32[]{:S(2)}, u32[]{:S(2)}) collective-permute-start(bf16[1280,80]{1,0:T(8,128)(2,1)} %collective-permute-done.12), channel_id=1, source_target_pairs={{0,32},{32,64},{64,96},{96,128},{128,160},{160,192},{192,224},{224... | collective-permute-start | bytes 614408 | tf_op jit(solution)/shard_map/ppermute | solution.py:23
  154.3 124.0 %all-to-all-start.1 = ((s32[4,32,1]{0,2,1:T(1,128)}), s32[4,32,1]{0,2,1:T(1,128)S(1)}, u32[]{:S(2)}, u32[]{:S(2)}) async-start(s32[4,32,1]{0,2,1:T(1,128)} %copy.47), calls=%async_computation.1 | async-start | bytes 32768 | tf_op jit(solution)/shard_map/all_to_all | solution.py:135
  195.8 39.8 %copy-start.16 = (f32[1280]{0:T(1024)S(1)}, f32[1280]{0:T(1024)}, u32[]{:S(2)}) copy-start(f32[1280]{0:T(1024)} %param.9) | copy-start | bytes 15364
  278.2 42.3 %all-to-all-start.3 = ((bf16[4,32,5120]{2,0,1:T(4,128)(2,1)}), bf16[4,32,5120]{2,0,1:T(4,128)(2,1)S(1)}, u32[]{:S(2)}, u32[]{:S(2)}) async-start(bf16[4,32,5120]{2,0,1:T(4,128)(2,1)} %copy.54), calls=%async_computation.3 | async-start | bytes 2621440 | tf_op jit(solution)/shard_map/all_to_all | solution.py:134
  (5 other events, 11.7 us)
Sparse Core Ops, SparseCore 0:
  39.8 65.9 all-gather.1
